TPU v7x, 32 devices: a whole 2x2x4 slice. The times are simulated.
32 devices in a mesh: dm: 4 (over z), tm: 8 (over y, x, core).
Axes of the slice: x: 2, y: 2, z: 4, core: 2. Of those that a mesh axis runs over, the one named last changes fastest.
Arguments:
- dispersed: float32 [1024, 8192], P('dm', 'tm')
- widths: int32 [4], replicated, may hold values from 1 to 129, as said below
Outputs:
- snr: bfloat16 [4, 1024, 8192], P(None, 'dm', 'tm')
- peaks: float32 [4, 1024], P(None, 'dm')
Inputs may be any that keep to these rules, and one draw needn't show every extreme that they name: `widths`: at least one width equals 129.
All inputs are finite; a program needn't handle non-finite values.
Results may differ from a plain program's by a relative error of at most 0.001.
Values sent between devices are 32-bit elements; how exact they have to be, the bound alone decides.
A program may use at most 64 MiB of HBM per device.

v0:
```python
import jax
import jax.numpy as jnp
from jax import lax
from jax.sharding import PartitionSpec as P

HALF = 128
eps_value = 1e-06


def with_halo(x, sides, width):
    for axis, dim in sides:
        peers, length = (lax.axis_size(axis), x.shape[dim])
        up = [(i, (i + 1) % peers) for i in range(peers - 1)]
        down = [(j, i) for i, j in up]
        last = lax.slice_in_dim(x, length - width, length, axis=dim)
        leading = lax.slice_in_dim(x, 0, width, axis=dim)
        before = lax.ppermute(last, axis, up)
        after = lax.ppermute(leading, axis, down)
        x = jnp.concatenate([before, x, after], axis=dim)
    return x


def from_behind(block, axis, distance):
    devices = range(lax.axis_size(axis))
    route = [(i - distance, i) for i in devices if i - distance in devices]
    return lax.ppermute(block, axis, route)


def band_table(span_list, block_len):
    column_idx = jnp.arange(span_list.shape[0] * block_len, dtype=jnp.int32)
    offsets = column_idx % block_len
    reaches = jnp.repeat(span_list, block_len)
    row_idx = jnp.arange(2 * block_len, dtype=jnp.int32)[:, None]
    inside = (row_idx >= offsets[None, :]) & (row_idx < offsets[None, :] + reaches[None, :])
    return inside.astype(jnp.float32)


def window_sum(extended, length, band_matrix, block_len):
    row_count = extended.shape[0]
    block_count = length // block_len
    blocks = extended.reshape(row_count, block_count + 1, block_len)
    paired = jnp.concatenate([blocks[:, :-1], blocks[:, 1:]], axis=2)
    return jnp.einsum("rbs,sk->rbk", paired, band_matrix, precision=lax.Precision.HIGHEST)


def boxcar(extended, length, band_matrix, inverse, block_len):
    row_count = extended.shape[0]
    moving = window_sum(extended, length, band_matrix, block_len)
    moving = moving.reshape(row_count, length // block_len, inverse.shape[0], block_len)
    moving = jnp.transpose(moving, (2, 0, 1, 3)).reshape(inverse.shape[0], row_count, length)
    return moving * inverse[:, None, None]


def body(dispersed, widths):
    row_count, length = dispersed.shape
    block_len = 2 * HALF
    total_len = length * lax.axis_size("tm")
    offset = lax.axis_index("tm") * length
    ma_band = band_table(jnp.full((1,), 2 * HALF + 1, jnp.int32), block_len)
    box_band = band_table(widths, block_len)
    inverse = 1.0 / jnp.sqrt(widths.astype(jnp.float32))

    def counts_at(first_pos, size_len):
        positions = first_pos + jnp.arange(size_len, dtype=jnp.int32)
        counts = (
            jnp.minimum(positions + HALF, total_len - 1) - jnp.maximum(positions - HALF, 0) + 1
        ).astype(jnp.float32)
        inside = (positions >= 0) & (positions < total_len)
        return (counts, inside)

    local_counts = counts_at(offset, length)[0]
    extended = with_halo(dispersed, (("tm", 1),), 2 * HALF)
    wide_counts, inside = counts_at(offset - HALF, length + block_len)
    first_mean = window_sum(extended, length + block_len, ma_band, block_len).reshape(
        row_count, length + block_len
    )
    widened = jnp.where(inside[None, :], first_mean / wide_counts, 0.0)
    smooth_mean = (
        window_sum(widened, length, ma_band, block_len).reshape(row_count, length) / local_counts
    )
    detrended = dispersed - smooth_mean
    padding = jnp.zeros((row_count, HALF), jnp.float32)
    power_sum = lax.psum(jnp.sum(detrended * detrended, axis=1), "tm")
    row_spread_scale = jnp.sqrt(power_sum / total_len + eps_value)
    normed = detrended / row_spread_scale[:, None]
    colsum = lax.psum(jnp.sum(normed, axis=0), "dm")
    cleaned = normed - (colsum / (row_count * lax.axis_size("dm")))[None, :]
    head_cols = from_behind(cleaned[:, :HALF], "tm", -1)
    series = boxcar(
        jnp.concatenate([cleaned, head_cols, padding], axis=1), length, box_band, inverse, block_len
    )
    peak_values = lax.pmax(jnp.max(series, axis=2), "tm")
    return (series.astype(jnp.bfloat16), peak_values)


def solution(mesh):
    placed = (P("dm", "tm"), P())
    return jax.shard_map(
        body,
        mesh=mesh,
        in_specs=placed,
        out_specs=(P(None, "dm", "tm"), P(None, "dm")),
        check_vma=False,
    )
```

profile of v0, /device:TPU:4, one launch (start us, length us, event | category | flops | bytes accessed | tf_op | source)
XLA Modules:
  0.0 113.8 jit_solution(7534095986708861592)
XLA Ops:
  0.6 1.6 %copy.23 = f32[256,1024]{0,1:T(8,128)S(1)} copy(f32[256,1024]{1,0:T(8,128)} %param.2) | data formatting | bytes 2097152 | tf_op args[0]
  2.3 1.9 %collective-permute-start = (f32[256,256]{0,1:T(8,128)S(1)}, f32[256,256]{0,1:T(8,128)S(1)}, u32[]{:S(2)}, u32[]{:S(2)}) collective-permute-start(f32[256,256]{0,1:T(8,128)S(1)} %get-tuple-element.12), channel_id=1, source_target_pairs={{0,1},{1,2},{2,3},{3,4},{4,5},{5,6},{6,7},{8,9},{9,10},{10,11},{11... | collective-permute-start | bytes 786440 | tf_op jit(solution)/shard_map/ppermute | solution.py:17
  4.2 4.5 %collective-permute-start.1 = (f32[256,256]{0,1:T(8,128)S(1)}, f32[256,256]{0,1:T(8,128)S(1)}, u32[]{:S(2)}, u32[]{:S(2)}) collective-permute-start(f32[256,256]{0,1:T(8,128)S(1)} %get-tuple-element.13), channel_id=1, source_target_pairs={{1,0},{2,1},{3,2},{4,3},{5,4},{6,5},{7,6},{9,8},{10,9},{11,10},{12... | collective-permute-start | bytes 786440 | tf_op jit(solution)/shard_map/ppermute | solution.py:18
  8.8 0.1 broadcast_bitcast_fusion
  8.9 2.0 %collective-permute-done = f32[256,256]{0,1:T(8,128)S(1)} collective-permute-done((f32[256,256]{0,1:T(8,128)S(1)}, f32[256,256]{0,1:T(8,128)S(1)}, u32[]{:S(2)}, u32[]{:S(2)}) %collective-permute-start) | collective-permute-done | bytes 262176 | tf_op jit(solution)/shard_map/ppermute | solution.py:17
  10.9 1.7 %collective-permute-done.1 = f32[256,256]{0,1:T(8,128)S(1)} collective-permute-done((f32[256,256]{0,1:T(8,128)S(1)}, f32[256,256]{0,1:T(8,128)S(1)}, u32[]{:S(2)}, u32[]{:S(2)}) %collective-permute-start.1) | collective-permute-done | bytes 262176 | tf_op jit(solution)/shard_map/ppermute | solution.py:18
  12.6 0.1 pad_maximum_fusion
  12.7 1.3 %fusion.40 = (f32[256,5,256]{0,2,1:T(8,128)}, f32[256,5,256]{0,2,1:T(8,128)S(1)}) fusion(f32[256,6,256]{0,2,1:T(8,128)S(1)} %bitcast.22), kind=kLoop, calls=%fused_computation.58 | loop fusion | bytes 5242880 | tf_op jit(solution)/shard_map/slice | solution.py:42
  14.0 2.8 %copy.29 = f32[256,5,256]{2,0,1:T(8,128)} copy(f32[256,5,256]{0,2,1:T(8,128)} %get-tuple-element.6) | data formatting | bytes 2621440
  16.8 1.5 %copy.30 = f32[256,5,256]{2,0,1:T(8,128)} copy(f32[256,5,256]{0,2,1:T(8,128)S(1)} %get-tuple-element.7) | data formatting | bytes 2621440
  18.2 3.4 %divide_select_fusion = f32[256,5,256]{0,2,1:T(8,128)S(1)} fusion(f32[256,5,256]{2,0,1:T(8,128)} %copy.30, f32[256,5,256]{2,0,1:T(8,128)} %copy.29, f32[5,256]{1,0:T(8,128)S(1)} %add_convert_fusion, pred[5,256]{1,0:T(8,128)(4,1)S(1)} %fusion.31, s32[256]{0:T(256)S(1)} %get-tuple-element.15, s32[256]{0:T(256)S(1)} %get-tuple-element.14), kind=kOutput, calls=%fused_computation.20 | convolution fusion | flops 2014969856 | bytes 3940608 | tf_op jit(solution)/shard_map/rbs,sk->rbk/dot_general | solution.py:43
  21.6 0.2 fusion.42
  21.8 1.3 %fusion.4 = f32[256,4,256]{0,2,1:T(8,128)S(1)} fusion(f32[256,4,256]{0,2,1:T(8,128)S(1)} %get-tuple-element.11, f32[256,4,256]{0,2,1:T(8,128)S(1)} %get-tuple-element.10, s32[256]{0:T(256)S(1)} %get-tuple-element.15, s32[256]{0:T(256)S(1)} %get-tuple-element.14), kind=kOutput, calls=%fused_computation.6 | convolution fusion | flops 1611530240 | bytes 3147776 | tf_op jit(solution)/shard_map/rbs,sk->rbk/dot_general | solution.py:43
  23.1 0.3 multiply_reduce_fusion.1
  23.4 14.6 %psum.14 = f32[256]{0:T(256)S(1)} all-reduce(f32[256]{0:T(256)S(1)} %get-tuple-element.4), channel_id=1, replica_groups=mesh['dm'=4,'tm'=8] {'tm'}, use_global_device_ids=true, to_apply=%region_1.2 | all-reduce | flops 256 | bytes 2048 | tf_op jit(solution)/shard_map/psum | solution.py:83
  38.0 0.2 fusion.22
  38.2 12.0 %psum.15 = f32[1024]{0:T(1024)S(1)} all-reduce(f32[1024]{0:T(1024)S(1)} %fusion.22), channel_id=1, replica_groups=mesh['dm'=4,'tm'=8] {'dm'}, use_global_device_ids=true, to_apply=%region_3.4 | all-reduce | flops 1024 | bytes 8192 | tf_op jit(solution)/shard_map/psum | solution.py:86
  50.2 0.2 broadcast_subtract_fusion
  50.4 1.9 %collective-permute-start.2 = (f32[256,128]{0,1:T(8,128)S(1)}, f32[256,128]{0,1:T(8,128)S(1)}, u32[]{:S(2)}, u32[]{:S(2)}) collective-permute-start(f32[256,128]{0,1:T(8,128)S(1)} %slice.42), channel_id=1, source_target_pairs={{1,0},{2,1},{3,2},{4,3},{5,4},{6,5},{7,6},{9,8},{10,9},{11,10},{12... | collective-permute-start | bytes 393224 | tf_op jit(solution)/shard_map/ppermute | solution.py:26
  52.4 2.5 %collective-permute-done.2 = f32[256,128]{0,1:T(8,128)S(1)} collective-permute-done((f32[256,128]{0,1:T(8,128)S(1)}, f32[256,128]{0,1:T(8,128)S(1)}, u32[]{:S(2)}, u32[]{:S(2)}) %collective-permute-start.2) | collective-permute-done | bytes 131104 | tf_op jit(solution)/shard_map/ppermute | solution.py:26
  54.9 0.2 maximum_maximum_fusion
  55.1 0.2 fusion.41
  55.3 0.3 copy.31
  55.6 0.3 copy.32
  56.0 5.2 %fusion.8 = f32[256,4,1024]{2,0,1:T(8,128)} fusion(f32[256,4,256]{2,0,1:T(8,128)S(1)} %copy.32, f32[256,4,256]{2,0,1:T(8,128)S(1)} %copy.31, s32[1024]{0:T(1024)S(1)} %get-tuple-element.17, s32[1024]{0:T(1024)S(1)} %get-tuple-element.16), kind=kOutput, calls=%fused_computation.10 | convolution fusion | flops 6444548096 | bytes 6299648 | tf_op jit(solution)/shard_map/rbs,sk->rbk/dot_general | solution.py:43
  61.2 5.6 %reshape.95 = f32[256,4,4,256]{3,2,0,1:T(4,128)} reshape(f32[256,4,1024]{2,0,1:T(8,128)} %fusion.8) | data formatting | bytes 8388608 | tf_op jit(solution)/shard_map/reshape | solution.py:49
  66.8 3.2 %multiply_reduce_fusion = f32[4,256]{0,1:T(8,128)S(1)} fusion(f32[4]{0:T(128)S(1)} %convert_rsqrt_fusion, f32[256,4,4,256]{3,2,0,1:T(4,128)} %reshape.95), kind=kLoop, calls=%fused_computation | loop fusion | flops 2096128 | bytes 4198416 | tf_op jit(solution)/shard_map/reduce_max | solution.py:92
  70.0 26.4 %pmax.7 = f32[4,256]{0,1:T(8,128)S(1)} all-reduce(f32[4,256]{0,1:T(8,128)S(1)} %multiply_reduce_fusion), channel_id=1, replica_groups=mesh['dm'=4,'tm'=8] {'tm'}, use_global_device_ids=true, to_apply=%region_5.6 | all-reduce | flops 1024 | bytes 8192 | tf_op jit(solution)/shard_map/pmax | solution.py:92
  96.4 0.7 copy.27
  97.0 6.9 %copy.26 = f32[4,256,4,256]{3,2,1,0:T(4,128)} copy(f32[4,256,4,256]{3,0,1,2:T(4,128)} %bitcast.21) | data formatting | bytes 8388608 | tf_op jit(solution)/shard_map/transpose | solution.py:50
  103.9 5.8 %reshape.96 = f32[4,256,1024]{2,1,0:T(8,128)} reshape(f32[4,256,4,256]{3,2,1,0:T(4,128)} %copy.26) | data formatting | bytes 8388608 | tf_op jit(solution)/shard_map/reshape | solution.py:50
  109.7 4.1 %multiply_convert_fusion = bf16[4,256,1024]{2,1,0:T(8,128)(2,1)} fusion(f32[4,256,1024]{2,1,0:T(8,128)} %reshape.96, f32[4]{0:T(128)S(1)} %convert_rsqrt_fusion), kind=kLoop, calls=%fused_computation.1 | loop fusion | flops 2097152 | bytes 6291472 | tf_op jit(solution)/shard_map/convert_element_type | solution.py:93
  (15 shorter events, 0.1 us)
Async XLA Ops:
  0.6 8.2 %copy-start = (s32[4]{0:T(128)S(1)}, s32[4]{0:T(128)}, u32[]{:S(2)}) copy-start(s32[4]{0:T(128)} %param.3) | copy-start | bytes 52
  2.3 8.7 %collective-permute-start = (f32[256,256]{0,1:T(8,128)S(1)}, f32[256,256]{0,1:T(8,128)S(1)}, u32[]{:S(2)}, u32[]{:S(2)}) collective-permute-start(f32[256,256]{0,1:T(8,128)S(1)} %get-tuple-element.12), channel_id=1, source_target_pairs={{0,1},{1,2},{2,3},{3,4},{4,5},{5,6},{6,7},{8,9},{9,10},{10,11},{11... | collective-permute-start | bytes 786440 | tf_op jit(solution)/shard_map/ppermute | solution.py:17
  4.2 8.4 %collective-permute-start.1 = (f32[256,256]{0,1:T(8,128)S(1)}, f32[256,256]{0,1:T(8,128)S(1)}, u32[]{:S(2)}, u32[]{:S(2)}) collective-permute-start(f32[256,256]{0,1:T(8,128)S(1)} %get-tuple-element.13), channel_id=1, source_target_pairs={{1,0},{2,1},{3,2},{4,3},{5,4},{6,5},{7,6},{9,8},{10,9},{11,10},{12... | collective-permute-start | bytes 786440 | tf_op jit(solution)/shard_map/ppermute | solution.py:18
  50.4 4.4 %collective-permute-start.2 = (f32[256,128]{0,1:T(8,128)S(1)}, f32[256,128]{0,1:T(8,128)S(1)}, u32[]{:S(2)}, u32[]{:S(2)}) collective-permute-start(f32[256,128]{0,1:T(8,128)S(1)} %slice.42), channel_id=1, source_target_pairs={{1,0},{2,1},{3,2},{4,3},{5,4},{6,5},{7,6},{9,8},{10,9},{11,10},{12... | collective-permute-start | bytes 393224 | tf_op jit(solution)/shard_map/ppermute | solution.py:26
where the time goes:
time: 114 us
  blocking collectives  53 us (46%)
  local copies, waits for them, and re-layouts  27.2 us (24%)
  matrix products  9.89 us (9%)
  other arithmetic  8.4 us (7%)
  starting transfers between devices  8.38 us (7%)
  waiting for transfers between devices  6.19 us (5%)
    pmax x1, blocking collectives, body(): peak_values = lax.pmax(jnp.max(series, axis=2), 'tm')  26.4 us
    psum x1, blocking collectives, body(): power_sum = lax.psum(jnp.sum(detrended * detrended, axis=1), 'tm')  14.6 us
    psum x1, blocking collectives, body(): colsum = lax.psum(jnp.sum(normed, axis=0), 'dm')  12 us
    dot_general x3, matrix products, window_sum(): jnp.einsum('rbs,sk->rbk', paired, band_matrix, precision=lax.Precision.HI...  9.89 us
    unnamed x10, local copies, waits for them, and re-layouts  7.21 us
    transpose x1, local copies, waits for them, and re-layouts, boxcar(): jnp.transpose(moving, (2, 0, 1, 3))  6.85 us
    reshape x1, local copies, waits for them, and re-layouts, boxcar(): jnp.transpose(moving, (2, 0, 1, 3))  5.78 us
    reshape x1, local copies, waits for them, and re-layouts, boxcar(): moving.reshape(row_count, length // block_len, inverse.shape[0], block_len)  5.62 us
  transfers between devices with their start and end apart: 3, of which 3 were waited for; matrix products, arithmetic and copies ran while one was open for 0% of the time, Pallas kernels for 0%

commit v1 on v0

--- a/solution.py
+++ b/solution.py
@@ -5,6 +5,11 @@
 
 HALF = 128
 eps_value = 1e-06
+
+
+def summed_here(x, name):
+    parts = lax.all_gather(x, name)
+    return jnp.sum(parts, axis=0)
 
 
 def with_halo(x, sides, width):
@@ -80,7 +85,7 @@
     )
     detrended = dispersed - smooth_mean
     padding = jnp.zeros((row_count, HALF), jnp.float32)
-    power_sum = lax.psum(jnp.sum(detrended * detrended, axis=1), "tm")
+    power_sum = summed_here(jnp.sum(detrended * detrended, axis=1), "tm")
     row_spread_scale = jnp.sqrt(power_sum / total_len + eps_value)
     normed = detrended / row_spread_scale[:, None]
     colsum = lax.psum(jnp.sum(normed, axis=0), "dm")

time: 114 us -> 109 us (0.956)
  blocking collectives: 53 us -> 47.5 us
    psum x1 -> x0, blocking collectives: 14.6 us -> none  [body(): power_sum = lax.psum(jnp.sum(detrended * detrended, axis=1), 'tm')]
    all_gather x0 -> x1, blocking collectives: none -> 9.15 us  [summed_here(): parts = lax.all_gather(x, name)]
where the time goes in v1:
time: 109 us; the launch traced here: 108 us
  blocking collectives  47.5 us (44%)
  local copies, waits for them, and re-layouts  27.2 us (25%)
  matrix products  9.89 us (9%)
  other arithmetic  8.43 us (8%)
  starting transfers between devices  8.38 us (8%)
  waiting for transfers between devices  6.19 us (6%)
    pmax x1, blocking collectives, body(): peak_values = lax.pmax(jnp.max(series, axis=2), 'tm')  26.4 us
    psum x1, blocking collectives, body(): colsum = lax.psum(jnp.sum(normed, axis=0), 'dm')  12 us
    dot_general x3, matrix products, window_sum(): jnp.einsum('rbs,sk->rbk', paired, band_matrix, precision=lax.Precision.HI...  9.89 us
    all_gather x1, blocking collectives, summed_here(): parts = lax.all_gather(x, name)  9.15 us
    unnamed x10, local copies, waits for them, and re-layouts  7.21 us
    transpose x1, local copies, waits for them, and re-layouts, boxcar(): jnp.transpose(moving, (2, 0, 1, 3))  6.85 us
    reshape x1, local copies, waits for them, and re-layouts, boxcar(): jnp.transpose(moving, (2, 0, 1, 3))  5.78 us
    reshape x1, local copies, waits for them, and re-layouts, boxcar(): moving.reshape(row_count, length // block_len, inverse.shape[0], block_len)  5.62 us
  transfers between devices with their start and end apart: 3, of which 3 were waited for; matrix products, arithmetic and copies ran while one was open for 0% of the time, Pallas kernels for 0%

profile of v1, /device:TPU:4, one launch (start us, length us, event | category | flops | bytes accessed | tf_op | source)
XLA Modules:
  0.0 108.4 jit_solution(3340712182863165493)
XLA Ops:
  0.6 1.6 %copy.23 = f32[256,1024]{0,1:T(8,128)S(1)} copy(f32[256,1024]{1,0:T(8,128)} %param.2) | data formatting | bytes 2097152 | tf_op args[0]
  2.3 1.9 %collective-permute-start = (f32[256,256]{0,1:T(8,128)S(1)}, f32[256,256]{0,1:T(8,128)S(1)}, u32[]{:S(2)}, u32[]{:S(2)}) collective-permute-start(f32[256,256]{0,1:T(8,128)S(1)} %get-tuple-element.12), channel_id=1, source_target_pairs={{0,1},{1,2},{2,3},{3,4},{4,5},{5,6},{6,7},{8,9},{9,10},{10,11},{11... | collective-permute-start | bytes 786440 | tf_op jit(solution)/shard_map/ppermute | solution.py:22
  4.2 4.5 %collective-permute-start.1 = (f32[256,256]{0,1:T(8,128)S(1)}, f32[256,256]{0,1:T(8,128)S(1)}, u32[]{:S(2)}, u32[]{:S(2)}) collective-permute-start(f32[256,256]{0,1:T(8,128)S(1)} %get-tuple-element.13), channel_id=1, source_target_pairs={{1,0},{2,1},{3,2},{4,3},{5,4},{6,5},{7,6},{9,8},{10,9},{11,10},{12... | collective-permute-start | bytes 786440 | tf_op jit(solution)/shard_map/ppermute | solution.py:23
  8.8 0.1 broadcast_bitcast_fusion
  8.9 2.0 %collective-permute-done = f32[256,256]{0,1:T(8,128)S(1)} collective-permute-done((f32[256,256]{0,1:T(8,128)S(1)}, f32[256,256]{0,1:T(8,128)S(1)}, u32[]{:S(2)}, u32[]{:S(2)}) %collective-permute-start) | collective-permute-done | bytes 262176 | tf_op jit(solution)/shard_map/ppermute | solution.py:22
  10.9 1.7 %collective-permute-done.1 = f32[256,256]{0,1:T(8,128)S(1)} collective-permute-done((f32[256,256]{0,1:T(8,128)S(1)}, f32[256,256]{0,1:T(8,128)S(1)}, u32[]{:S(2)}, u32[]{:S(2)}) %collective-permute-start.1) | collective-permute-done | bytes 262176 | tf_op jit(solution)/shard_map/ppermute | solution.py:23
  12.6 0.1 pad_maximum_fusion
  12.7 1.3 %fusion.40 = (f32[256,5,256]{0,2,1:T(8,128)}, f32[256,5,256]{0,2,1:T(8,128)S(1)}) fusion(f32[256,6,256]{0,2,1:T(8,128)S(1)} %bitcast.23), kind=kLoop, calls=%fused_computation.58 | loop fusion | bytes 5242880 | tf_op jit(solution)/shard_map/slice | solution.py:47
  14.0 2.8 %copy.29 = f32[256,5,256]{2,0,1:T(8,128)} copy(f32[256,5,256]{0,2,1:T(8,128)} %get-tuple-element.6) | data formatting | bytes 2621440
  16.8 1.5 %copy.30 = f32[256,5,256]{2,0,1:T(8,128)} copy(f32[256,5,256]{0,2,1:T(8,128)S(1)} %get-tuple-element.7) | data formatting | bytes 2621440
  18.2 3.4 %divide_select_fusion = f32[256,5,256]{0,2,1:T(8,128)S(1)} fusion(f32[256,5,256]{2,0,1:T(8,128)} %copy.30, f32[256,5,256]{2,0,1:T(8,128)} %copy.29, f32[5,256]{1,0:T(8,128)S(1)} %add_convert_fusion, pred[5,256]{1,0:T(8,128)(4,1)S(1)} %fusion.31, s32[256]{0:T(256)S(1)} %get-tuple-element.15, s32[256]{0:T(256)S(1)} %get-tuple-element.14), kind=kOutput, calls=%fused_computation.20 | convolution fusion | flops 2014969856 | bytes 3940608 | tf_op jit(solution)/shard_map/rbs,sk->rbk/dot_general | solution.py:48
  21.6 0.2 fusion.42
  21.8 1.3 %fusion.4 = f32[256,4,256]{0,2,1:T(8,128)S(1)} fusion(f32[256,4,256]{0,2,1:T(8,128)S(1)} %get-tuple-element.11, f32[256,4,256]{0,2,1:T(8,128)S(1)} %get-tuple-element.10, s32[256]{0:T(256)S(1)} %get-tuple-element.15, s32[256]{0:T(256)S(1)} %get-tuple-element.14), kind=kOutput, calls=%fused_computation.6 | convolution fusion | flops 1611530240 | bytes 3147776 | tf_op jit(solution)/shard_map/rbs,sk->rbk/dot_general | solution.py:48
  23.1 0.3 multiply_reduce_fusion.1
  23.4 9.1 %all-gather.1 = f32[8,1,256]{2,1,0:T(1,128)S(1)} all-gather(f32[1,1,256]{2,1,0:T(1,128)S(1)} %bitcast.26), channel_id=2, replica_groups=mesh['dm'=4,'tm'=8] {'tm'}, dimensions={0}, use_global_device_ids=true | all-gather | bytes 9216 | tf_op jit(solution)/shard_map/all_gather | solution.py:11
  32.6 0.2 fusion.22
  32.8 12.0 %psum.7 = f32[1024]{0:T(1024)S(1)} all-reduce(f32[1024]{0:T(1024)S(1)} %fusion.22), channel_id=1, replica_groups=mesh['dm'=4,'tm'=8] {'dm'}, use_global_device_ids=true, to_apply=%region_3.4 | all-reduce | flops 1024 | bytes 8192 | tf_op jit(solution)/shard_map/psum | solution.py:91
  44.8 0.2 broadcast_subtract_fusion
  45.0 1.9 %collective-permute-start.2 = (f32[256,128]{0,1:T(8,128)S(1)}, f32[256,128]{0,1:T(8,128)S(1)}, u32[]{:S(2)}, u32[]{:S(2)}) collective-permute-start(f32[256,128]{0,1:T(8,128)S(1)} %slice.42), channel_id=1, source_target_pairs={{1,0},{2,1},{3,2},{4,3},{5,4},{6,5},{7,6},{9,8},{10,9},{11,10},{12... | collective-permute-start | bytes 393224 | tf_op jit(solution)/shard_map/ppermute | solution.py:31
  47.0 2.5 %collective-permute-done.2 = f32[256,128]{0,1:T(8,128)S(1)} collective-permute-done((f32[256,128]{0,1:T(8,128)S(1)}, f32[256,128]{0,1:T(8,128)S(1)}, u32[]{:S(2)}, u32[]{:S(2)}) %collective-permute-start.2) | collective-permute-done | bytes 131104 | tf_op jit(solution)/shard_map/ppermute | solution.py:31
  49.4 0.2 maximum_maximum_fusion
  49.7 0.2 fusion.41
  49.9 0.3 copy.31
  50.2 0.3 copy.32
  50.5 5.2 %fusion.8 = f32[256,4,1024]{2,0,1:T(8,128)} fusion(f32[256,4,256]{2,0,1:T(8,128)S(1)} %copy.32, f32[256,4,256]{2,0,1:T(8,128)S(1)} %copy.31, s32[1024]{0:T(1024)S(1)} %get-tuple-element.17, s32[1024]{0:T(1024)S(1)} %get-tuple-element.16), kind=kOutput, calls=%fused_computation.10 | convolution fusion | flops 6444548096 | bytes 6299648 | tf_op jit(solution)/shard_map/rbs,sk->rbk/dot_general | solution.py:48
  55.7 5.6 %reshape.99 = f32[256,4,4,256]{3,2,0,1:T(4,128)} reshape(f32[256,4,1024]{2,0,1:T(8,128)} %fusion.8) | data formatting | bytes 8388608 | tf_op jit(solution)/shard_map/reshape | solution.py:54
  61.4 3.2 %multiply_reduce_fusion = f32[4,256]{0,1:T(8,128)S(1)} fusion(f32[4]{0:T(128)S(1)} %convert_rsqrt_fusion, f32[256,4,4,256]{3,2,0,1:T(4,128)} %reshape.99), kind=kLoop, calls=%fused_computation | loop fusion | flops 2096128 | bytes 4198416 | tf_op jit(solution)/shard_map/reduce_max | solution.py:97
  64.6 26.4 %pmax.7 = f32[4,256]{0,1:T(8,128)S(1)} all-reduce(f32[4,256]{0,1:T(8,128)S(1)} %multiply_reduce_fusion), channel_id=1, replica_groups=mesh['dm'=4,'tm'=8] {'tm'}, use_global_device_ids=true, to_apply=%region_5.6 | all-reduce | flops 1024 | bytes 8192 | tf_op jit(solution)/shard_map/pmax | solution.py:97
  90.9 0.7 copy.27
  91.6 6.9 %copy.26 = f32[4,256,4,256]{3,2,1,0:T(4,128)} copy(f32[4,256,4,256]{3,0,1,2:T(4,128)} %bitcast.22) | data formatting | bytes 8388608 | tf_op jit(solution)/shard_map/transpose | solution.py:55
  98.5 5.8 %reshape.100 = f32[4,256,1024]{2,1,0:T(8,128)} reshape(f32[4,256,4,256]{3,2,1,0:T(4,128)} %copy.26) | data formatting | bytes 8388608 | tf_op jit(solution)/shard_map/reshape | solution.py:55
  104.2 4.1 %multiply_convert_fusion = bf16[4,256,1024]{2,1,0:T(8,128)(2,1)} fusion(f32[4,256,1024]{2,1,0:T(8,128)} %reshape.100, f32[4]{0:T(128)S(1)} %convert_rsqrt_fusion), kind=kLoop, calls=%fused_computation.1 | loop fusion | flops 2097152 | bytes 6291472 | tf_op jit(solution)/shard_map/convert_element_type | solution.py:98
  (16 shorter events, 0.2 us)
Async XLA Ops:
  0.6 8.2 %copy-start = (s32[4]{0:T(128)S(1)}, s32[4]{0:T(128)}, u32[]{:S(2)}) copy-start(s32[4]{0:T(128)} %param.3) | copy-start | bytes 52
  2.3 8.7 %collective-permute-start = (f32[256,256]{0,1:T(8,128)S(1)}, f32[256,256]{0,1:T(8,128)S(1)}, u32[]{:S(2)}, u32[]{:S(2)}) collective-permute-start(f32[256,256]{0,1:T(8,128)S(1)} %get-tuple-element.12), channel_id=1, source_target_pairs={{0,1},{1,2},{2,3},{3,4},{4,5},{5,6},{6,7},{8,9},{9,10},{10,11},{11... | collective-permute-start | bytes 786440 | tf_op jit(solution)/shard_map/ppermute | solution.py:22
  4.2 8.4 %collective-permute-start.1 = (f32[256,256]{0,1:T(8,128)S(1)}, f32[256,256]{0,1:T(8,128)S(1)}, u32[]{:S(2)}, u32[]{:S(2)}) collective-permute-start(f32[256,256]{0,1:T(8,128)S(1)} %get-tuple-element.13), channel_id=1, source_target_pairs={{1,0},{2,1},{3,2},{4,3},{5,4},{6,5},{7,6},{9,8},{10,9},{11,10},{12... | collective-permute-start | bytes 786440 | tf_op jit(solution)/shard_map/ppermute | solution.py:23
  45.0 4.4 %collective-permute-start.2 = (f32[256,128]{0,1:T(8,128)S(1)}, f32[256,128]{0,1:T(8,128)S(1)}, u32[]{:S(2)}, u32[]{:S(2)}) collective-permute-start(f32[256,128]{0,1:T(8,128)S(1)} %slice.42), channel_id=1, source_target_pairs={{1,0},{2,1},{3,2},{4,3},{5,4},{6,5},{7,6},{9,8},{10,9},{11,10},{12... | collective-permute-start | bytes 393224 | tf_op jit(solution)/shard_map/ppermute | solution.py:31
